TPU v7x, 8 devices: a whole 2x2x1 slice. The times are simulated.
8 devices in a mesh: stage: 4 (over z, y, x), tp: 2 (over core).
Axes of the slice: x: 2, y: 2, z: 1, core: 2. Of those that a mesh axis runs over, the one named last changes fastest.
Arguments:
- x: bfloat16 [4, 4096, 1536], P(None, 'tp')
- g: bfloat16 [4, 2, 1536], P('stage')
- w1: bfloat16 [4, 2, 1536, 6144], P('stage', None, None, 'tp')
- w2: bfloat16 [4, 2, 6144, 1536], P('stage', None, 'tp')
Outputs:
- output: bfloat16 [4, 4, 4096, 1536], P('stage', None, 'tp')
All inputs are finite; a program needn't handle non-finite values.
Results may differ from a plain program's by a relative error of at most 0.0197235.
Values are sent between devices in bfloat16 or wider.
A program may use at most 1 GiB of HBM per device.

v0:
```python
import functools

import jax
import jax.numpy as jnp
from jax import lax
from jax.experimental import pallas as pl
from jax.experimental.pallas import tpu as pltpu
from jax.sharding import PartitionSpec as P

EPS = 1e-5
C = 144
NS = 4
NO = 3
TP = 4
LR = 24
T = 256
EARLY = 2


def _gelu(u):
    k0 = 0.7978845608028654
    k1 = k0 * 0.044715
    return u * (0.5 + 0.5 * jnp.tanh(u * (k0 + k1 * (u * u))))


def _kernel(S, R, D, FH, x, g, w1, w2, y,
            w1v, w2v, gv, gf, ybuf, ob, h, a, pb, pr,
            rs, ss, osem, otail, yr, xs, wl, wrs, wrr, gs, ps, prs, credit, pair, seen):
    KT, NH = D // T, FH // T
    NT = 2 * NH
    NP, N2 = NT // 2, KT // 2
    NV, W = w1v.shape[1], w1v.shape[3]
    HC = -(-R // C)
    OV = HC * C - R
    NC = 2 * HC
    LX = NS
    B = C - OV

    p = lax.axis_index('stage')
    i = lax.axis_index('tp')
    j = 2 * p + i
    last = 2 * S - 1
    has_prev, has_next = j > 0, j < last
    odd = i == 1
    prv = (lax.rem(p + S - 1 + i, S), 1 - i)
    nxt = (lax.rem(p + i, S), 1 - i)
    partner = (p, 1 - i)
    MESH = pl.DeviceIdType.MESH

    def rows(q, skip=0, n=C):
        r = lax.rem(q, HC)
        at = r * C - lax.div(r, HC - 1) * OV + skip
        return pl.ds(pl.multiple_of(at, 16), n)

    def arrival(q):
        s = lax.rem(q, NS)
        return pltpu.make_async_copy(x.at[rows(q), :], ybuf.at[s], rs.at[s])

    def send(q):
        so, s = lax.rem(q, NO), lax.rem(q, NS)
        return pltpu.make_async_remote_copy(ob.at[so], ybuf.at[s], ss.at[so], rs.at[s], device_id=nxt, device_id_type=MESH)

    def xpush(q):
        s = lax.rem(q, NS)
        return pltpu.make_async_remote_copy(x.at[rows(q), :], ybuf.at[s], xs.at[0], rs.at[s], device_id=prv, device_id_type=MESH)

    def xfeed(q):
        return pltpu.make_async_remote_copy(x.at[rows(q), :], ybuf.at[q], xs.at[0], rs.at[q], device_id=nxt, device_id_type=MESH)

    def out_local(q):
        so = lax.rem(q, NO)
        return pltpu.make_async_copy(ob.at[so, pl.ds(OV, B)], y.at[rows(q, OV, B), :], osem.at[so])

    def out_remote(q):
        so = lax.rem(q, NO)
        return pltpu.make_async_remote_copy(ob.at[so, pl.ds(OV, B)], y.at[rows(q, OV, B), :], osem.at[so], yr.at[0],
                                            device_id=partner, device_id_type=MESH)

    def tail_local(q):
        so = lax.rem(q, NO)
        return pltpu.make_async_copy(ob.at[so, pl.ds(0, OV)], y.at[rows(q, 0, OV), :], otail.at[so])

    def tail_remote(q):
        so = lax.rem(q, NO)
        return pltpu.make_async_remote_copy(ob.at[so, pl.ds(0, OV)], y.at[rows(q, 0, OV), :], otail.at[so], yr.at[0],
                                            device_id=partner, device_id_type=MESH)

    def whole(q):
        return lax.rem(q, HC) < HC - 1

    def base(b):
        return 2 * lax.rem(b + i, 2)

    def deep(third):
        return pl.ds(pl.multiple_of(third * FH, T), FH)

    def load(b):
        r1, r2 = D // 2, FH // 4
        return [pltpu.make_async_copy(w1.at[0, b, pl.ds(r * r1, r1), pl.ds(v * W, W)], w1v.at[base(b), v, pl.ds(r * r1, r1), :], wl.at[b])
                for v in range(NV) for r in range(2)] + [
            pltpu.make_async_copy(w2.at[0, b, pl.ds(r * r2, r2), :],
                                  w2v.at[pl.ds(pl.multiple_of(base(b) * FH + r * r2, 16), r2), :], wl.at[2 + b]) for r in range(4)]

    D4, F4 = D // (4 // NV), FH // 4

    def give1(t):
        at = lax.rem(t, 4 // NV), lax.div(t, 4 // NV)
        r, v = pl.ds(pl.multiple_of(at[0] * D4, 16), D4), at[1]
        return pltpu.make_async_remote_copy(w1.at[0, 1 - i, r, pl.ds(pl.multiple_of(v * W, T), W)], w1v.at[1, v, r, :],
                                            wrs.at[0], wrr.at[0], device_id=partner, device_id_type=MESH)

    def give2(t):
        r = lax.rem(t, 4) * F4
        return pltpu.make_async_remote_copy(w2.at[0, 1 - i, pl.ds(pl.multiple_of(r, 16), F4), :],
                                            w2v.at[pl.ds(pl.multiple_of(FH + r, 16), F4), :],
                                            wrs.at[1], wrr.at[1], device_id=partner, device_id_type=MESH)

    half1, half2 = w1v.at[1], w2v.at[pl.ds(0, FH), :]
    got1, sent1 = (pltpu.make_async_copy(half1, half1, sem) for sem in (wrr.at[0], wrs.at[0]))
    got2, sent2 = (pltpu.make_async_copy(half2, half2, sem) for sem in (wrr.at[1], wrs.at[1]))

    def own1(b):
        pltpu.make_async_copy(half1, half1, wl.at[b]).wait()

    def own2(b):
        pltpu.make_async_copy(half2, half2, wl.at[2 + b]).wait()

    def own(b):
        own1(b)
        own2(b)

    def cols1(third, n):
        v, at = divmod(2 * n * T, W)
        return w1v[third, v, :, at:at + 2 * T]

    gcopy = pltpu.make_async_copy(g.at[0], gv, gs.at[0])

    bar = pltpu.get_barrier_semaphore()

    @pl.when(has_prev)
    def _():
        pl.semaphore_signal(bar, 1, device_id=prv, device_id_type=MESH)

    @pl.when(has_next)
    def _():
        pl.semaphore_signal(bar, 1, device_id=nxt, device_id_type=MESH)

    gcopy.start()

    @pl.when(j == 0)
    def _():
        for q in range(LX):
            arrival(q).start()

    for b in range(2):
        @pl.when((i == b) & (p > 0) if b else (p == 0) | (i == b))
        def _():
            for cp in load(b):
                cp.start()

    @pl.when(has_prev & has_next)
    def _():
        pl.semaphore_wait(bar, 2)

    @pl.when((j == 0) | (j == last))
    def _():
        pl.semaphore_wait(bar, 1)

    @pl.when(j == 0)
    def _():
        for q in range(TP):
            xfeed(q).start()

    for t in range(EARLY):
        give1(jnp.int32(t)).start()

    @pl.when(p > 0)
    def _():
        for t in range(EARLY, 4):
            give1(jnp.int32(t)).start()
        for t in range(4):
            give2(jnp.int32(t)).start()

    @pl.when(has_prev)
    def _():
        pl.semaphore_signal(credit, NS, device_id=prv, device_id_type=MESH)


    gcopy.wait()
    for b in range(2):
        gf[b] = gv[b:b + 1, :].astype(jnp.float32)

    def ln(s, b):
        for r in range(0, C, LR):
            yf = ybuf[s, r:r + LR, :].astype(jnp.float32)
            mu = jnp.mean(yf, axis=-1, keepdims=True)
            d = yf - mu
            var = jnp.mean(jnp.square(d), axis=-1, keepdims=True)
            hh = (d * lax.rsqrt(var + EPS) * gf[b]).astype(jnp.bfloat16)
            for k in range(KT):
                h[k, r:r + LR, :] = hh[:, k * T:(k + 1) * T]

    def mm1(n):
        lhs = jnp.concatenate([h[k] for k in range(KT)], axis=1)
        rhs = cols1(n // (NP // 2), n % (NP // 2))
        t = jnp.dot(lhs, rhs, preferred_element_type=jnp.float32)
        for u in range(2):
            a[2 * n + u] = _gelu(t[:, u * T:(u + 1) * T]).astype(jnp.bfloat16)

    def mm2(n, q):
        s, so = lax.rem(q, NS), lax.rem(q, NO)
        lhs = jnp.concatenate([a[k] for k in range(NT)], axis=1)
        rhs = w2v[:2 * FH, 2 * n * T:2 * (n + 1) * T]
        t = jnp.dot(lhs, rhs, preferred_element_type=jnp.float32)
        cols = slice(2 * n * T, 2 * (n + 1) * T)
        ob[so, :, cols] = (ybuf[s, :, cols].astype(jnp.float32) + t).astype(jnp.bfloat16)

    def slot_free(q, ok=True):
        @pl.when(ok & has_next & ((j > 0) | (q >= TP)))
        def _():
            send(q).wait_send()

        @pl.when(ok & odd)
        def _():
            out_local(q).wait()

        if OV:
            @pl.when(ok & odd & whole(q))
            def _():
                tail_local(q).wait()

    def put_out(q, sends):
        @pl.when(has_next)
        def _():
            pl.semaphore_wait(credit, 1)

        @pl.when(has_prev)
        def _():
            pl.semaphore_signal(credit, 1, device_id=prv, device_id_type=MESH)

        @pl.when(sends)
        def _():
            send(q).start()

        @pl.when(odd & (q < HC))
        def _():
            out_remote(q).start()

        @pl.when(odd & (q >= HC))
        def _():
            out_local(q).start()

        if OV:
            @pl.when(odd & (q < HC) & whole(q))
            def _():
                tail_remote(q).start()

            @pl.when(odd & (q >= HC) & whole(q))
            def _():
                tail_local(q).start()

        @pl.when((j == 0) & (q + LX < HC))
        def _():
            arrival(q + LX).start()

        @pl.when((j == 1) & (q + LX > HC) & (q + LX < NC))
        def _():
            xpush(q + LX - 1).wait_send()

        @pl.when((j == 1) & (q + LX >= HC) & (q + LX < NC))
        def _():
            xpush(q + LX).start()

    def partial(q, b):
        return pltpu.make_async_remote_copy(pb.at[lax.rem(q, 2)], pr.at[lax.rem(q, 2)], ps.at[lax.rem(q, 2)],
                                            prs.at[lax.rem(q, 2) + 2 * b], device_id=partner, device_id_type=MESH)

    def both(q):
        k = lax.rem(q, 2)
        return pb[k].astype(jnp.float32) + pr[k].astype(jnp.float32)

    def split(t, _):
        b, q = lax.rem(lax.div(t, 2), 2), 2 * lax.div(t, 4) + lax.rem(t, 2)
        k, s = lax.rem(q, 2), lax.rem(q, NS)

        @pl.when(t == 0)
        def _():
            own(0)
            for cp in load(1):
                cp.start()

        @pl.when(t == 2)
        def _():
            own(1)

        @pl.when(b == 0)
        def _():
            arrival(q).wait()

        @pl.when(b == 1)
        def _():
            partial(q, 0).wait_recv()
            ybuf[s] = (ybuf[s].astype(jnp.float32) + both(q)).astype(jnp.bfloat16)

        @pl.when((b == 1) & odd)
        def _():
            pl.semaphore_signal(seen, 1, device_id=partner, device_id_type=MESH)

        @pl.when((b == 1) | ((t >= 4) & (i == 0)))
        def _():
            partial(q, b).wait_send()

        ln(s, b)
        for n in range(NH // 2):
            lhs = jnp.concatenate([h[k2] for k2 in range(KT)], axis=1)
            rhs = cols1(base(b), n)
            u = jnp.dot(lhs, rhs, preferred_element_type=jnp.float32)
            for v in range(2):
                a[2 * n + v] = _gelu(u[:, v * T:(v + 1) * T]).astype(jnp.bfloat16)
        for n in range(N2):
            lhs = jnp.concatenate([a[k2] for k2 in range(NH)], axis=1)
            rhs = w2v[deep(base(b)), 2 * n * T:2 * (n + 1) * T]
            u = jnp.dot(lhs, rhs, preferred_element_type=jnp.float32)
            pb[k, :, 2 * n * T:2 * (n + 1) * T] = u.astype(jnp.bfloat16)

        @pl.when((i == 0) & (lax.rem(t, 4) == 0) & (t >= 4))
        def _():
            pl.semaphore_wait(pair, 1)

        @pl.when((b == 1) & (i == 0))
        def _():
            pl.semaphore_wait(seen, 1)

        @pl.when((b == 0) | (i == 0))
        def _():
            partial(q, b).start()

        @pl.when(t + EARLY < 4)
        def _():
            give1(t + EARLY).start()

        @pl.when((t + EARLY >= 4) & (t + EARLY < 8))
        def _():
            give2(t + EARLY).start()

        def go_out(q):
            slot_free(q - NO, odd & (q >= NO))

            @pl.when(odd)
            def _():
                partial(q, 1).wait_recv()
                ob[lax.rem(q, NO)] = (ybuf[lax.rem(q, NS)].astype(jnp.float32) + both(q)).astype(jnp.bfloat16)
            put_out(q, odd)

        @pl.when(lax.rem(t, 4) == 3)
        def _():
            go_out(q - 1)
            go_out(q)

        @pl.when(odd & (lax.rem(t, 4) == 3) & (t < 2 * TP - 1))
        def _():
            pl.semaphore_signal(pair, 1, device_id=partner, device_id_type=MESH)
        return 0

    @pl.when(p == 0)
    def _():
        lax.fori_loop(0, 2 * TP, split, 0)

        @pl.when(i == 0)
        def _():
            for q in (TP - 2, TP - 1):
                partial(jnp.int32(q), 1).wait_send()
            pltpu.make_async_copy(x.at[pl.ds(0, TP * C), :], x.at[pl.ds(0, TP * C), :], xs.at[0]).wait()

        @pl.when(odd)
        def _():
            slot_free(jnp.int32(TP - NO))

    @pl.when(p > 0)
    def _():
        own(i)
    got1.wait()
    got2.wait()
    first = jnp.where(p == 0, TP, 0)
    arrival(first).wait()

    def body(q, _):
        ln(lax.rem(q, NS), i)
        for n in range(NP):
            mm1(n)
        for n in range(N2):
            mm2(n, q)
        put_out(q, has_next)

        @pl.when(q + 1 < NC)
        def _():
            arrival(q + 1).wait()
        slot_free(q + 1 - NO, q + 1 >= NO)
        return 0

    lax.fori_loop(first, NC, body, 0)

    for d in range(1, NO):
        slot_free(jnp.int32(NC - NO + d))

    @pl.when(has_next)
    def _():
        pl.semaphore_wait(credit, NS)

    @pl.when(j == 1)
    def _():
        xpush(jnp.int32(NC - 1)).wait_send()

    sent1.wait()
    sent2.wait()

    @pl.when(i == 0)
    def _():
        pltpu.make_async_copy(y, y, yr.at[0]).wait()


def _move(n, src, dst, buf, isem, osem):
    b = src.shape[0] // n
    into = [pltpu.make_async_copy(src.at[pl.ds(k * b, b), :], buf.at[pl.ds(k * b, b), :], isem.at[k]) for k in range(n)]
    outof = [pltpu.make_async_copy(buf.at[pl.ds(k * b, b), :], dst.at[pl.ds(k * b, b), :], osem.at[k]) for k in range(n)]
    for cp in into:
        cp.start()
    for k in range(n):
        into[k].wait()
        outof[k].start()
    for cp in outof:
        cp.wait()


def solution(mesh):
    S = mesh.shape['stage']

    def local(x, g, w1, w2):
        M, TL, D = x.shape
        FH = w1.shape[-1]
        bf = jnp.bfloat16
        dma = pltpu.SemaphoreType.DMA
        out = pl.pallas_call(
            functools.partial(_kernel, S, M * TL, D, FH),
            out_shape=jax.ShapeDtypeStruct((M * TL, D), bf),
            in_specs=[pl.BlockSpec(memory_space=pl.ANY)] * 4,
            out_specs=pl.BlockSpec(memory_space=pl.ANY),
            scratch_shapes=[
                pltpu.VMEM((3, 2, D, FH // 2), bf),
                pltpu.VMEM((3 * FH, D), bf),
                pltpu.VMEM((2, D), bf),
                pltpu.VMEM((2, 1, D), jnp.float32),
                pltpu.VMEM((NS, C, D), bf),
                pltpu.VMEM((NO, C, D), bf),
                pltpu.VMEM((D // T, C, T), bf),
                pltpu.VMEM((2 * FH // T, C, T), bf),
                pltpu.VMEM((2, C, D), bf),
                pltpu.VMEM((2, C, D), bf),
                dma((NS,)), dma((NO,)), dma((NO,)), dma((NO,)), dma((1,)), dma((1,)),
                dma((4,)), dma((2,)), dma((2,)), dma((1,)), dma((2,)), dma((4,)),
                pltpu.SemaphoreType.REGULAR, pltpu.SemaphoreType.REGULAR, pltpu.SemaphoreType.REGULAR,
            ],
            compiler_params=pltpu.CompilerParams(
                collective_id=0, has_side_effects=True, vmem_limit_bytes=67043328),
            cost_estimate=pl.CostEstimate(flops=8 * M * TL * D * 2 * FH, bytes_accessed=4 * M * TL * D, transcendentals=0),
        )(x.reshape(M * TL, D), g, w1, w2)
        n = 16
        out = pl.pallas_call(
            functools.partial(_move, n),
            out_shape=jax.ShapeDtypeStruct(out.shape, out.dtype),
            in_specs=[pl.BlockSpec(memory_space=pl.ANY)],
            out_specs=pl.BlockSpec(memory_space=pl.ANY),
            scratch_shapes=[pltpu.VMEM(out.shape, out.dtype), dma((n,)), dma((n,))],
            compiler_params=pltpu.CompilerParams(vmem_limit_bytes=67043328),
        )(out)
        return out.reshape(1, M, TL, D)

    return jax.shard_map(
        local, mesh=mesh,
        in_specs=(P(None, 'tp', None), P('stage', None, None),
                  P('stage', None, None, 'tp'), P('stage', None, 'tp', None)),
        out_specs=P('stage', None, 'tp', None), check_vma=False)
```

profile of v0, /device:TPU:7, one launch (start us, length us, event | category | flops | bytes accessed | tf_op | source)
XLA Modules:
  0.0 780.5 jit_solution(17983695404755798741)
XLA Ops:
  0.0 763.2 %shard_map.46.src = bf16[8192,1536]{1,0:T(8,128)(2,1)} custom-call(bf16[8192,1536]{1,0:T(8,128)(2,1)} %bitcast.2, bf16[1,2,1536]{2,1,0:T(2,128)(2,1)} %g.1, bf16[1,2,1536,3072]{3,2,1,0:T(8,128)(2,1)} %w1.1, bf16[1,2,3072,1536]{3,2,1,0:T(8,128)(2,1)} %w2.1), custom_call_target="tpu_custom_call" | custom-call | flops 618475290624 | bytes 50331648 | tf_op jit(solution)/shard_map/pallas_call | solution.py:443
  763.2 17.3 %shard_map.47 = bf16[8192,1536]{1,0:T(8,128)(2,1)} custom-call(bf16[8192,1536]{1,0:T(8,128)(2,1)} %shard_map.46.src), custom_call_target="tpu_custom_call" | custom-call | tf_op jit(solution)/shard_map/pallas_call | solution.py:468
where the time goes:
time: 781 us
  Pallas kernels  781 us (100%)
    pallas_call x1, Pallas kernels, local(): pl.pallas_call(functools.partial(_kernel, S, M * TL, D, FH), out_shape=ja...  763 us
    pallas_call x1, Pallas kernels, local(): pl.pallas_call(functools.partial(_move, n), out_shape=jax.ShapeDtypeStruc...  17.3 us

commit v1 on v0

--- a/solution.py
+++ b/solution.py
@@ -229,39 +229,35 @@
             def _():
                 tail_local(q).wait()
 
-    def put_out(q, sends):
+    def put_out(q, sends, half):
         @pl.when(has_next)
         def _():
             pl.semaphore_wait(credit, 1)
 
+            if sends is True:
+                send(q).start()
+            else:
+                @pl.when(sends)
+                def _():
+                    send(q).start()
+
         @pl.when(has_prev)
         def _():
             pl.semaphore_signal(credit, 1, device_id=prv, device_id_type=MESH)
 
-        @pl.when(sends)
-        def _():
-            send(q).start()
-
-        @pl.when(odd & (q < HC))
-        def _():
-            out_remote(q).start()
-
-        @pl.when(odd & (q >= HC))
-        def _():
-            out_local(q).start()
+        @pl.when(odd)
+        def _():
+            (out_local if half else out_remote)(q).start()
 
         if OV:
-            @pl.when(odd & (q < HC) & whole(q))
+            @pl.when(odd & whole(q))
             def _():
-                tail_remote(q).start()
-
-            @pl.when(odd & (q >= HC) & whole(q))
+                (tail_local if half else tail_remote)(q).start()
+
+        if not half:
+            @pl.when((j == 0) & (q + LX < HC))
             def _():
-                tail_local(q).start()
-
-        @pl.when((j == 0) & (q + LX < HC))
-        def _():
-            arrival(q + LX).start()
+                arrival(q + LX).start()
 
         @pl.when((j == 1) & (q + LX > HC) & (q + LX < NC))
         def _():
@@ -350,7 +346,7 @@
             def _():
                 partial(q, 1).wait_recv()
                 ob[lax.rem(q, NO)] = (ybuf[lax.rem(q, NS)].astype(jnp.float32) + both(q)).astype(jnp.bfloat16)
-            put_out(q, odd)
+            put_out(q, odd, 0)
 
         @pl.when(lax.rem(t, 4) == 3)
         def _():
@@ -384,13 +380,13 @@
     first = jnp.where(p == 0, TP, 0)
     arrival(first).wait()
 
-    def body(q, _):
+    def body(half, q, _):
         ln(lax.rem(q, NS), i)
         for n in range(NP):
             mm1(n)
         for n in range(N2):
             mm2(n, q)
-        put_out(q, has_next)
+        put_out(q, True, half)
 
         @pl.when(q + 1 < NC)
         def _():
@@ -398,7 +394,8 @@
         slot_free(q + 1 - NO, q + 1 >= NO)
         return 0
 
-    lax.fori_loop(first, NC, body, 0)
+    lax.fori_loop(first, min(HC, NC), functools.partial(body, 0), 0)
+    lax.fori_loop(HC, max(HC, NC), functools.partial(body, 1), 0)
 
     for d in range(1, NO):
         slot_free(jnp.int32(NC - NO + d))
@@ -427,6 +424,7 @@
         cp.start()
     for k in range(n):
         into[k].wait()
+    for k in range(n):
         outof[k].start()
     for cp in outof:
         cp.wait()
@@ -464,7 +462,7 @@
                 collective_id=0, has_side_effects=True, vmem_limit_bytes=67043328),
             cost_estimate=pl.CostEstimate(flops=8 * M * TL * D * 2 * FH, bytes_accessed=4 * M * TL * D, transcendentals=0),
         )(x.reshape(M * TL, D), g, w1, w2)
-        n = 16
+        n = 8
         out = pl.pallas_call(
             functools.partial(_move, n),
             out_shape=jax.ShapeDtypeStruct(out.shape, out.dtype),

time: 781 us -> 780 us (level)
  no operation moved by 1% of the time
where the time goes in v1:
time: 780 us
  Pallas kernels  780 us (100%)
    pallas_call x1, Pallas kernels, local(): pl.pallas_call(functools.partial(_kernel, S, M * TL, D, FH), out_shape=ja...  763 us
    pallas_call x1, Pallas kernels, local(): pl.pallas_call(functools.partial(_move, n), out_shape=jax.ShapeDtypeStruc...  16.8 us

profile of v1, /device:TPU:7, one launch (start us, length us, event | category | flops | bytes accessed | tf_op | source)
XLA Modules:
  0.0 780.1 jit_solution(122015820993894721)
XLA Ops:
  0.0 763.1 %shard_map.46.src = bf16[8192,1536]{1,0:T(8,128)(2,1)} custom-call(bf16[8192,1536]{1,0:T(8,128)(2,1)} %bitcast.2, bf16[1,2,1536]{2,1,0:T(2,128)(2,1)} %g.1, bf16[1,2,1536,3072]{3,2,1,0:T(8,128)(2,1)} %w1.1, bf16[1,2,3072,1536]{3,2,1,0:T(8,128)(2,1)} %w2.1), custom_call_target="tpu_custom_call" | custom-call | flops 618475290624 | bytes 50331648 | tf_op jit(solution)/shard_map/pallas_call | solution.py:441
  763.1 16.8 %shard_map.47 = bf16[8192,1536]{1,0:T(8,128)(2,1)} custom-call(bf16[8192,1536]{1,0:T(8,128)(2,1)} %shard_map.46.src), custom_call_target="tpu_custom_call" | custom-call | tf_op jit(solution)/shard_map/pallas_call | solution.py:466
